TPU v7x, 32 devices: a whole 2x2x4 slice. The times are simulated.
32 devices in a mesh: tp: 2 (over x), dp: 4 (over y, core), rep: 4 (over z).
Axes of the slice: x: 2, y: 2, z: 4, core: 2. Of those that a mesh axis runs over, the one named last changes fastest.
Arguments:
- prompts: bfloat16 [12288, 8192], P(('dp', 'rep'), 'tp'), may hold values from -6 to 6
- frozen_projection_weight: bfloat16 [2, 8192, 2048], P(None, ('dp', 'rep'), 'tp'), may hold values from -5 to 5
- lowrank_down_factor: bfloat16 [2, 8192, 64], P(None, ('dp', 'rep')), may hold values from -0.119628906 to 0.119628906
- lowrank_up_factor: bfloat16 [2, 64, 2048], P(None, None, 'tp'), may hold values from -0.59765625 to 0.59765625
- magnitude: float32 [2, 2048], P(None, 'tp'), may hold values from 0.5 to 2
Outputs:
- key_values: bfloat16 [2, 12288, 2048], P(None, ('dp', 'rep'), 'tp')
All inputs are finite; a program needn't handle non-finite values.
Results may differ from a plain program's by a relative error of at most 0.0049.
Values may be sent and summed in bfloat16 or wider, within the bound.
A program may use at most 128 MiB of HBM per device.

v0:
```python
import functools

import jax
import jax.numpy as jnp
from jax import lax
from jax.experimental import pallas as pl
from jax.experimental.pallas import tpu as pltpu
from jax.sharding import PartitionSpec as P

epsilon = 1e-06
MESH = pl.DeviceIdType.MESH


def merge_rows(weight_rows, down_rows, up_matrix):
    return weight_rows.astype(jnp.float32) + jnp.einsum(
        "lrk,lkc->lrc", down_rows, up_matrix, preferred_element_type=jnp.float32
    )


def kernel(
    sizes, prompts_ref, merged_ref, acc, squares,
    wbuf, pbuf,
    arrive, zsend, zown, ysend, csend, psend, parrive, load_p, load_w,
):
    tp_size, dp_size, rep_size = sizes
    y_size = dp_size // 2
    layers, rows, columns = merged_ref.shape
    groups = dp_size // tp_size
    x = lax.axis_index("tp")
    d = lax.axis_index("dp")
    z = lax.axis_index("rep")
    y, c = d // 2, lax.rem(d, 2)
    partner = {"tp": x, "dp": d + 1 - 2 * c, "rep": z}

    early = rows * 5 // 16
    pieces = [(0, 0, early), (0, early, rows - early)]
    for layer in range(1, layers):
        pieces += [(layer, 0, rows // 2), (layer, rows // 2, rows // 2)]
    count = len(pieces)

    def block(yy, cc, zz):
        return (yy * 2 + cc) * rep_size + zz

    def piece(b, s):
        layer, start, size = pieces[s]
        return wbuf.at[b, layer, pl.ds(start, size), :]

    pending = []

    def send(cond, ref, send_sem, recv_sem, device):
        def make():
            return pltpu.make_async_remote_copy(
                src_ref=ref, dst_ref=ref, send_sem=send_sem, recv_sem=recv_sem,
                device_id=device, device_id_type=MESH,
            )

        pending.append((cond, make))
        if cond is None:
            make().start()
        else:
            @pl.when(cond)
            def _():
                make().start()

    def wait_piece(b, s):
        pltpu.make_async_remote_copy(
            src_ref=piece(b, s), dst_ref=piece(b, s), send_sem=csend.at[0],
            recv_sem=arrive.at[b * count + s], device_id=partner, device_id_type=MESH,
        ).wait_recv()

    def z_device(step):
        return {"tp": x, "dp": d, "rep": z + step}

    def y_device(o):
        return {"tp": x, "dp": lax.rem(y + o, y_size) * 2 + c, "rep": z}

    def to_partner(cond, yy, zz, s):
        b = block(yy, c, zz)
        send(cond, piece(b, s), csend.at[(yy * rep_size + zz) * count + s], arrive.at[b * count + s], partner)

    def to_y(cond, zz, s):
        b = block(y, c, zz)
        for o in range(1, y_size):
            send(
                cond, piece(b, s), ysend.at[((o - 1) * rep_size + zz) * count + s],
                arrive.at[b * count + s], y_device(o),
            )

    def along_z(cond, yy, zz, s, step):
        b = block(yy, c, zz)
        send(
            cond, piece(b, s), zsend.at[(yy * rep_size + zz) * count + s],
            arrive.at[b * count + s], z_device(step),
        )

    def start_z(yy, s):
        b = block(yy, c, z)
        send(z < rep_size - 1, piece(b, s), zown.at[yy * count + s], arrive.at[b * count + s], z_device(1))
        along_z(z > 0, yy, z, s, -1)

    def when(cond, body):
        if cond is None:
            body()
        else:
            pl.when(cond)(body)

    me = block(y, c, z)
    load_weight = pltpu.make_async_copy(merged_ref, wbuf.at[me], load_w)
    load_weight.start()

    table = [sorted(range(rep_size), key=lambda k: (abs(k - at), k)) for at in range(rep_size)]

    def nearest(i):
        value = jnp.int32(table[0][i])
        for at in range(1, rep_size):
            value = jnp.where(z == at, jnp.int32(table[at][i]), value)
        return value

    own_chunks = []
    for i in range(rep_size):
        for g in range(groups):
            own_chunks.append((g * rep_size + nearest(i), x * groups * rep_size + g * rep_size + nearest(i)))

    def load_chunk(j, b):
        start = pl.multiple_of(j * rows, rows)
        return pltpu.make_async_copy(prompts_ref.at[:, pl.ds(start, rows)], pbuf.at[b], load_p.at[b])

    for j, b in own_chunks:
        load_chunk(j, b).start()

    barrier = pltpu.get_barrier_semaphore()
    pl.semaphore_signal(barrier, 1, device_id=partner, device_id_type=MESH)
    for o in range(1, y_size):
        pl.semaphore_signal(barrier, 1, device_id=y_device(o), device_id_type=MESH)
    for o in range(1, tp_size):
        pl.semaphore_signal(
            barrier, 1, device_id={"tp": lax.rem(x + o, tp_size), "dp": d, "rep": z}, device_id_type=MESH
        )

    @pl.when(z > 0)
    def _():
        pl.semaphore_signal(barrier, 1, device_id=z_device(-1), device_id_type=MESH)

    @pl.when(z < rep_size - 1)
    def _():
        pl.semaphore_signal(barrier, 1, device_id=z_device(1), device_id_type=MESH)

    neighbours = jnp.where(z > 0, 1, 0) + jnp.where(z < rep_size - 1, 1, 0)
    pl.semaphore_wait(barrier, neighbours + (1 + y_size - 1 + tp_size - 1))

    load_weight.wait()
    for s in range(count):
        to_y(None, z, s)
        start_z(y, s)
    for j, b in own_chunks:
        load_chunk(j, b).wait()
        for o in range(1, tp_size):
            send(
                None, pbuf.at[b], psend.at[(o - 1) * dp_size * rep_size + b], parrive.at[b],
                {"tp": lax.rem(x + o, tp_size), "dp": d, "rep": z},
            )
    for s in range(count):
        to_partner(None, y, z, s)

    acc[...] = jnp.zeros_like(acc)
    squares[...] = jnp.zeros_like(squares)
    tile = min(256, columns)

    def wait_chunk(b):
        @pl.when(b // (groups * rep_size) != x)
        def _():
            pltpu.make_async_remote_copy(
                src_ref=pbuf.at[b], dst_ref=pbuf.at[b], send_sem=psend.at[0], recv_sem=parrive.at[b],
                device_id=partner, device_id_type=MESH,
            ).wait_recv()

    def compute(b, first, last):
        tiles = columns // tile

        def step(t, carry):
            layer = first + t // tiles
            at = pl.ds(pl.multiple_of(lax.rem(t, tiles) * tile, tile), tile)
            weight = wbuf[b, layer, :, at]
            acc[layer, :, at] += jnp.dot(pbuf[b], weight, preferred_element_type=jnp.float32)
            wide = weight.astype(jnp.float32)
            squares[layer, :, at] += jnp.sum((wide * wide).reshape(rows // 8, 8, tile), axis=0)
            return carry

        lax.fori_loop(0, (last - first) * tiles, step, 0)

    def held(layer):
        return [s for s in range(count) if pieces[s][0] == layer]

    def own_layer(zz, layer):
        mine, other = block(y, c, zz), block(y, 1 - c, zz)
        if layer == 0:
            wait_chunk(mine)
        compute(mine, layer, layer + 1)
        for s in held(layer):
            wait_piece(other, s)
        if layer == 0:
            wait_chunk(other)
        compute(other, layer, layer + 1)

    def own(zz):
        mine, other = block(y, c, zz), block(y, 1 - c, zz)
        wait_chunk(mine)
        compute(mine, 0, layers)
        for s in range(count):
            wait_piece(other, s)
        wait_chunk(other)
        compute(other, 0, layers)

    def across(zz):
        for o in range(1, y_size):
            yy = lax.rem(y + o, y_size)
            mine, other = block(yy, c, zz), block(yy, 1 - c, zz)
            for layer in range(layers):
                for s in held(layer):
                    if s > 0:
                        wait_piece(mine, s)
                        to_partner_plain(yy, zz, s)
                if layer == 0:
                    wait_chunk(mine)
                compute(mine, layer, layer + 1)
                for s in held(layer):
                    wait_piece(other, s)
                if layer == 0:
                    wait_chunk(other)
                compute(other, layer, layer + 1)

    def to_partner_plain(yy, zz, s):
        b = block(yy, c, zz)

        def make():
            return pltpu.make_async_remote_copy(
                src_ref=piece(b, s), dst_ref=piece(b, s), send_sem=csend.at[(yy * rep_size + zz) * count + s],
                recv_sem=arrive.at[b * count + s], device_id=partner, device_id_type=MESH,
            )

        make().start()

    def take(zz, s, step):
        onward = (z + step >= 0) & (z + step <= rep_size - 1)

        def arrived(yy):
            b = block(yy, c, zz)
            wait_piece(b, s)

            @pl.when(onward)
            def _():
                pltpu.make_async_remote_copy(
                    src_ref=piece(b, s), dst_ref=piece(b, s), send_sem=zsend.at[(yy * rep_size + zz) * count + s],
                    recv_sem=arrive.at[b * count + s], device_id=z_device(step), device_id_type=MESH,
                ).start()

        arrived(y)
        if s > 0:
            b = block(y, c, zz)
            for o in range(1, y_size):
                pltpu.make_async_remote_copy(
                    src_ref=piece(b, s), dst_ref=piece(b, s),
                    send_sem=ysend.at[((o - 1) * rep_size + zz) * count + s],
                    recv_sem=arrive.at[b * count + s], device_id=y_device(o), device_id_type=MESH,
                ).start()
        to_partner_plain(y, zz, s)
        if s == 0:
            for o in range(1, y_size):
                yy = lax.rem(y + o, y_size)
                arrived(yy)
                to_partner_plain(yy, zz, 0)

    for o in range(1, y_size):
        yy = lax.rem(y + o, y_size)
        wait_piece(block(yy, c, z), 0)
        start_z(yy, 0)
        to_partner(None, yy, z, 0)

    def sides(r):
        return ((z - r >= 0, z - r, 1), (z + r <= rep_size - 1, z + r, -1))

    far = jnp.maximum(z, rep_size - 1 - z)

    def each(r, cond, body):
        def run():
            if 2 * r <= rep_size - 1:
                for valid, zz, step in sides(r):
                    pl.when(valid)(functools.partial(body, zz, step))
            else:
                low = z - r >= 0
                body(jnp.where(low, z - r, z + r), jnp.where(low, 1, -1))

        pl.when(cond & (r <= far))(run)

    def take_all(r, some):
        for s in some:
            each(r, r <= far, lambda zz, step, s=s: take(zz, s, step))

    if rep_size > 1:
        take_all(1, range(count))
    own(z)
    across(z)
    if rep_size > 1:
        each(1, far == 1, lambda zz, step: own(zz))
    for r in range(2, rep_size):
        two = (z - (r - 1) >= 0) & (z + (r - 1) <= rep_size - 1)
        one = jnp.logical_not(two) & (r <= far)
        last = r == far
        take_all(r, range(2))
        each(r - 1, one, lambda zz, step: own(zz))
        take_all(r, range(2, count - 1))
        each(r - 1, one, lambda zz, step: across(zz))
        each(r, one & last, lambda zz, step: own_layer(zz, 0))
        take_all(r, range(count - 1, count))

        def rest(zz, step):
            for layer in range(1, layers):
                own_layer(zz, layer)

        each(r, one & last, rest)
        if 2 * (r - 1) <= rep_size - 1:
            both = two & (r <= far)
            each(r - 1, both, lambda zz, step: own(zz))
            each(r, both & last, lambda zz, step: own(zz))
            each(r - 1, both, lambda zz, step: across(zz))
    for r in range(1, rep_size):
        if any(max(at, rep_size - 1 - at) == r for at in range(rep_size)):
            each(r, far == r, lambda zz, step: across(zz))

    def drain(cond, make):
        when(cond, lambda: make().wait_send())

    for cond, make in pending:
        drain(cond, make)

    def sent(ref, sem):
        return pltpu.make_async_remote_copy(
            src_ref=ref, dst_ref=ref, send_sem=sem, recv_sem=arrive.at[0], device_id=partner, device_id_type=MESH
        )

    for r in range(1, rep_size):
        for valid, zz, step in sides(r):
            @pl.when(valid)
            def _(zz=zz, step=step):
                onward = (z + step >= 0) & (z + step <= rep_size - 1)
                for s in range(count):
                    for o in range(y_size):
                        yy = lax.rem(y + o, y_size)
                        at = (yy * rep_size + zz) * count + s
                        ref = piece(block(yy, c, zz), s)
                        sent(ref, csend.at[at]).wait_send()
                        if o == 0 or s == 0:
                            @pl.when(onward)
                            def _():
                                sent(ref, zsend.at[at]).wait_send()
                    if s > 0:
                        for o in range(1, y_size):
                            sent(
                                piece(block(y, c, zz), s), ysend.at[((o - 1) * rep_size + zz) * count + s]
                            ).wait_send()
    for o in range(1, y_size):
        yy = lax.rem(y + o, y_size)
        for s in range(1, count):
            sent(piece(block(yy, c, z), s), csend.at[(yy * rep_size + z) * count + s]).wait_send()


def local(sizes, prompts, frozen_projection_weight, lowrank_down_factor, lowrank_up_factor, magnitude):
    tp_size, dp_size, rep_size = sizes
    merged = merge_rows(frozen_projection_weight, lowrank_down_factor, lowrank_up_factor).astype(jnp.bfloat16)
    layers, rows, columns = merged.shape
    tokens = prompts.shape[0]
    blocks = dp_size * rep_size
    y_size = dp_size // 2
    count = 2 * layers
    dma = pltpu.SemaphoreType.DMA
    product, squares = pl.pallas_call(
        functools.partial(kernel, sizes),
        out_shape=(
            jax.ShapeDtypeStruct((layers, tokens, columns), jnp.float32),
            jax.ShapeDtypeStruct((layers, 8, columns), jnp.float32),
        ),
        in_specs=[
            pl.BlockSpec(memory_space=pl.ANY),
            pl.BlockSpec(memory_space=pl.ANY),
        ],
        out_specs=(pl.BlockSpec(memory_space=pltpu.VMEM), pl.BlockSpec(memory_space=pltpu.VMEM)),
        scratch_shapes=[
            pltpu.VMEM((blocks, layers, rows, columns), jnp.bfloat16),
            pltpu.VMEM((blocks, tokens, rows), jnp.bfloat16),
            dma((blocks * count,)),
            dma((y_size * rep_size * count,)),
            dma((y_size * count,)),
            dma((max(1, (y_size - 1) * rep_size * count),)),
            dma((y_size * rep_size * count,)),
            dma((max(1, (tp_size - 1) * blocks),)),
            dma((blocks,)),
            dma((blocks,)),
            dma(()),
        ],
        compiler_params=pltpu.CompilerParams(
            collective_id=0, has_side_effects=True, vmem_limit_bytes=66_000_000
        ),
        cost_estimate=pl.CostEstimate(
            flops=2 * layers * tokens * columns * rows * blocks, bytes_accessed=2 * blocks * rows * columns,
            transcendentals=0,
        ),
    )(prompts, merged)
    factor = magnitude / jnp.sqrt(jnp.sum(squares, axis=1) + epsilon)
    return (product * factor[:, None, :]).astype(jnp.bfloat16)


def solution(mesh):
    in_specs = (
        P(("dp", "rep"), "tp"),
        P(None, ("dp", "rep"), "tp"),
        P(None, ("dp", "rep"), None),
        P(None, None, "tp"),
        P(None, "tp"),
    )
    out_specs = P(None, ("dp", "rep"), "tp")
    sizes = tuple(mesh.shape[name] for name in ("tp", "dp", "rep"))
    return jax.shard_map(
        functools.partial(local, sizes), mesh=mesh, in_specs=in_specs, out_specs=out_specs, check_vma=False
    )
```

profile of v0, /device:TPU:1, one launch (start us, length us, event | category | flops | bytes accessed | tf_op | source)
XLA Modules:
  0.0 198.6 jit_solution(313526172988800252)
XLA Ops:
  0.0 0.0 copy-start
  0.0 0.9 copy-done
  1.0 3.7 %add_convert_fusion.merged_ref = bf16[2,512,1024]{2,1,0:T(8,128)(2,1)} fusion(bf16[2,512,1024]{2,1,0:T(8,128)(2,1)} %param.6, bf16[2,512,64]{1,2,0:T(8,128)(2,1)} %param.7, bf16[2,64,1024]{2,1,0:T(8,128)(2,1)S(1)} %copy-done), kind=kOutput, calls=%fused_computation.1 | convolution fusion | flops 137363456 | bytes 4587520 | tf_op jit(solution)/shard_map/lrk,lkc->lrc/dot_general | solution.py:15
  4.7 0.0 copy-start.1
  4.7 187.6 %shard_map.55 = (f32[2,768,1024]{2,1,0:T(8,128)}, f32[2,8,1024]{2,1,0:T(8,128)}) custom-call(bf16[768,4096]{1,0:T(8,128)(2,1)} %prompts_ref.1, bf16[2,512,1024]{2,1,0:T(8,128)(2,1)} %add_convert_fusion.merged_ref), custom_call_target="tpu_custom_call" | custom-call | flops 25769803776 | bytes 16777216 | tf_op jit(solution)/shard_map/pallas_call | solution.py:376
  192.3 0.9 reduce_sum.9
  193.2 0.0 copy-done.1
  193.2 5.4 %multiply_convert_fusion = bf16[2,768,1024]{2,1,0:T(8,128)(2,1)} fusion(f32[2,768,1024]{2,1,0:T(8,128)} %get-tuple-element.7, f32[2,1024]{1,0:T(2,128)S(1)} %rsqrt_multiply_fusion), kind=kLoop, calls=%fused_computation | loop fusion | flops 3145728 | bytes 9445376 | tf_op jit(solution)/shard_map/convert_element_type | solution.py:409
  (1 shorter events, 0.0 us)
Async XLA Ops:
  0.0 1.0 copy-start
  4.7 188.5 %copy-start.1 = (f32[2,1024]{1,0:T(2,128)S(1)}, f32[2,1024]{1,0:T(2,128)}, u32[]{:S(2)}) copy-start(f32[2,1024]{1,0:T(2,128)} %param.9) | copy-start | bytes 24580
where the time goes:
time: 199 us
  Pallas kernels  188 us (94%)
  other arithmetic  6.27 us (3%)
  matrix products  3.74 us (2%)
    pallas_call x1, Pallas kernels, local(): pl.pallas_call(functools.partial(kernel, sizes), out_shape=(jax.ShapeDtyp...  188 us
    convert_element_type x1, other arithmetic, local(): return (product * factor[:, None, :]).astype(jnp.bfloat16)  5.39 us

commit v1 on v0

v1 whole, which is shorter than its diff:
```python
import functools

import jax
import jax.numpy as jnp
from jax import lax
from jax.experimental import pallas as pl
from jax.experimental.pallas import tpu as pltpu
from jax.sharding import PartitionSpec as P

epsilon = 1e-06
MESH = pl.DeviceIdType.MESH


def kernel(
    sizes, prompts_ref, weight_ref, down_ref, up_ref, magnitude_ref, out_ref,
    wbuf, pbuf, dbuf, ubuf, acc, squares,
    arrive, zup, zdown, ysend, csend, psend, parrive, load_p, load_w, load_f,
):
    tp_size, dp_size, rep_size = sizes
    y_size = dp_size // 2
    layers, rows, columns = weight_ref.shape
    tokens = prompts_ref.shape[0]
    half = rows // 2
    count = 2 * layers
    groups = dp_size // tp_size
    x = lax.axis_index("tp")
    d = lax.axis_index("dp")
    z = lax.axis_index("rep")
    y, c = d // 2, lax.rem(d, 2)
    partner = {"tp": x, "dp": d + 1 - 2 * c, "rep": z}
    last = rep_size - 1
    middle = (z > 0) & (z < last)

    def column(o):
        return lax.rem(y + o, y_size)

    def block(yy, cc, zz):
        return (yy * 2 + cc) * rep_size + zz

    def piece(b, k):
        start = pl.multiple_of(k // layers * half, half)
        return wbuf.at[b, lax.rem(k, layers), pl.ds(start, half), :]

    def ranked(at):
        longer = -1 if at > last - at else 1
        return sorted(range(rep_size), key=lambda k: (abs(k - at), -longer * (k - at)))

    table = [ranked(at) for at in range(rep_size)]

    def plane(i):
        value = jnp.int32(0)
        for at in range(rep_size):
            for step in range(rep_size):
                value = jnp.where((z == at) & (i == step), jnp.int32(table[at][step]), value)
        return value

    def doubled(zz, k):
        return ((zz == 0) | (zz == last)) & (k >= layers)

    def y_device(o):
        return {"tp": x, "dp": column(o) * 2 + c, "rep": z}

    def z_device(step):
        return {"tp": x, "dp": d, "rep": z + step}

    def remote(ref, send_sem, recv_sem, device):
        return pltpu.make_async_remote_copy(
            src_ref=ref, dst_ref=ref, send_sem=send_sem, recv_sem=recv_sem,
            device_id=device, device_id_type=MESH,
        )

    def wait_piece(b, k):
        remote(piece(b, k), csend.at[0], arrive.at[b * count + k], partner).wait_recv()

    def copies(o, zz, k, act):
        yy = column(o)
        b = block(yy, c, zz)
        ref, landed = piece(b, k), arrive.at[b * count + k]
        at = (yy * rep_size + zz) * count + k
        onz = doubled(zz, k)
        along = onz if o > 0 else (z >= 0)

        @pl.when(along & (zz >= z) & (z > 0))
        def _():
            act(remote(ref, zdown.at[at], landed, z_device(-1)))

        @pl.when(along & (zz <= z) & (z < last))
        def _():
            act(remote(ref, zup.at[at], landed, z_device(1)))

        if o == 0:
            for p in range(1, y_size):
                @pl.when((zz == z) | jnp.logical_not(onz))
                def _(p=p):
                    act(remote(ref, ysend.at[((p - 1) * rep_size + zz) * count + k], landed, y_device(p)))

        act(remote(ref, csend.at[at], landed, partner))

    def forward(o, zz, k):
        copies(o, zz, k, lambda copy: copy.start())

    def duty(o, zz, k):
        wait_piece(block(column(o), c, zz), k)
        forward(o, zz, k)

    me = block(y, c, z)

    def load_weight(k):
        start = k // layers * half
        return pltpu.make_async_copy(
            weight_ref.at[k % layers, pl.ds(start, half), :], piece(me, jnp.int32(k)), load_w.at[k]
        )

    load_down = pltpu.make_async_copy(down_ref, dbuf, load_f.at[0])
    load_up = pltpu.make_async_copy(up_ref, ubuf, load_f.at[1])
    load_down.start()
    load_up.start()
    for k in range(count):
        load_weight(k).start()

    own_chunks = []
    for i in range(rep_size):
        for g in range(groups):
            zz = plane(i)
            own_chunks.append((g * rep_size + zz, x * groups * rep_size + g * rep_size + zz))

    def load_chunk(j, b):
        start = pl.multiple_of(j * rows, rows)
        return pltpu.make_async_copy(prompts_ref.at[:, pl.ds(start, rows)], pbuf.at[b], load_p.at[b])

    for j, b in own_chunks:
        load_chunk(j, b).start()

    barrier = pltpu.get_barrier_semaphore()
    pl.semaphore_signal(barrier, 1, device_id=partner, device_id_type=MESH)
    for o in range(1, y_size):
        pl.semaphore_signal(barrier, 1, device_id=y_device(o), device_id_type=MESH)
    for o in range(1, tp_size):
        pl.semaphore_signal(
            barrier, 1, device_id={"tp": lax.rem(x + o, tp_size), "dp": d, "rep": z}, device_id_type=MESH
        )

    @pl.when(z > 0)
    def _():
        pl.semaphore_signal(barrier, 1, device_id=z_device(-1), device_id_type=MESH)

    @pl.when(z < last)
    def _():
        pl.semaphore_signal(barrier, 1, device_id=z_device(1), device_id_type=MESH)

    load_down.wait()
    load_up.wait()
    tile = min(256, columns)

    def merge(k):
        layer, start = k % layers, k // layers * half
        load_weight(k).wait()

        def step(t, carry):
            at = pl.ds(pl.multiple_of(t * tile, tile), tile)
            low = lax.dot_general(
                dbuf[layer, :, pl.ds(start, half)], ubuf[layer, :, at], (((0,), (0,)), ((), ())),
                preferred_element_type=jnp.float32,
            )
            wide = wbuf[me, layer, pl.ds(start, half), at].astype(jnp.float32) + low
            wbuf[me, layer, pl.ds(start, half), at] = wide.astype(wbuf.dtype)
            return carry

        lax.fori_loop(0, columns // tile, step, 0)

    neighbours = jnp.where(z > 0, 1, 0) + jnp.where(z < last, 1, 0)

    def send_chunk(j, b, act):
        for o in range(1, tp_size):
            act(
                remote(
                    pbuf.at[b], psend.at[(o - 1) * dp_size * rep_size + b], parrive.at[b],
                    {"tp": lax.rem(x + o, tp_size), "dp": d, "rep": z},
                )
            )

    for k in range(count):
        merge(k)
        if k == 0:
            pl.semaphore_wait(barrier, neighbours + (1 + y_size - 1 + tp_size - 1))
        else:
            forward(0, z, jnp.int32(k - 1))
    for j, b in own_chunks[:1]:
        load_chunk(j, b).wait()
        send_chunk(j, b, lambda copy: copy.start())
    forward(0, z, jnp.int32(count - 1))
    for j, b in own_chunks[1:]:
        load_chunk(j, b).wait()
        send_chunk(j, b, lambda copy: copy.start())

    acc[...] = jnp.zeros_like(acc)
    squares[...] = jnp.zeros_like(squares)

    def wait_chunk(b):
        @pl.when(b // (groups * rep_size) != x)
        def _():
            remote(pbuf.at[b], psend.at[0], parrive.at[b], partner).wait_recv()

    def compute(b, k):
        layer = lax.rem(k, layers)
        at = pl.ds(pl.multiple_of(k // layers * half, half), half)
        weight = wbuf[b, layer, at, :]
        acc[layer] += jnp.dot(pbuf[b, :, at], weight, preferred_element_type=jnp.float32)
        wide = weight.astype(jnp.float32)
        squares[layer] += jnp.sum((wide * wide).reshape(half // 8, 8, columns), axis=0)

    def blocks_of(q, zz):
        return block(column(q // 2), lax.rem(c + q, 2), zz)

    def consume(zz, k, first, end, fresh):
        def step(q, carry):
            b = blocks_of(q, zz)
            if fresh is not None:
                @pl.when(fresh)
                def _():
                    wait_chunk(b)

            @pl.when(lax.rem(q, 2) == 1)
            def _():
                wait_piece(b, k)

            compute(b, k)
            return carry

        lax.fori_loop(first, end, step, 0)

    total = last * count

    def z_duty(j):
        zz, k = plane(1 + j // count), lax.rem(j, count)
        onz = doubled(zz, k)

        @pl.when(middle | jnp.logical_not(onz))
        def _():
            duty(0, zz, k)

        @pl.when(middle & onz)
        def _():
            for o in range(1, y_size):
                duty(o, zz, k)

    lead = jnp.where(middle, count, 0)

    def ahead(j, carry):
        z_duty(j)
        return carry

    lax.fori_loop(0, lead, ahead, 0)

    def substep(m, carry):
        i, k = m // count, lax.rem(m, count)

        @pl.when(m + lead < total)
        def _():
            z_duty(m + lead)

        zz = plane(i)

        @pl.when((i == 0) | jnp.logical_not(doubled(zz, k)))
        def _():
            for o in range(1, y_size):
                duty(o, zz, k)

        consume(zz, k, 0, 2 * y_size, k == 0)
        return carry

    lax.fori_loop(0, total, substep, 0)

    far = plane(last)
    for q in range(2 * y_size):
        wait_chunk(blocks_of(q, far))

    def early(k, carry):
        consume(far, k, 0, 2, None)
        return carry

    lax.fori_loop(0, layers, early, 0)
    band = min(128, tokens)

    def finish(layer, carry):
        def late(part, inner):
            o_first = jnp.where(part == 0, 0, 2)
            o_end = jnp.where(part == 0, 2, 2 * y_size)
            k = jnp.where(part == 2, layer, layers + layer)

            @pl.when((part == 0) & jnp.logical_not(middle))
            def _():
                duty(0, far, k)

            @pl.when((part == 2) | ((part == 1) & jnp.logical_not(middle)))
            def _():
                for o in range(1, y_size):
                    duty(o, far, k)

            consume(far, k, o_first, o_end, None)
            return inner

        lax.fori_loop(0, 3, late, 0)
        norm = jnp.sqrt(jnp.sum(squares[layer], axis=0, keepdims=True) + epsilon)
        factor = magnitude_ref[pl.ds(layer, 1), :] / norm

        def scale(t, inner):
            at = pl.ds(pl.multiple_of(t * band, band), band)
            out_ref[layer, at, :] = (acc[layer, at, :] * factor).astype(out_ref.dtype)
            return inner

        lax.fori_loop(0, tokens // band, scale, 0)
        return carry

    lax.fori_loop(0, layers, finish, 0)

    def drain(t, carry):
        for o in range(y_size):
            copies(o, t // count, lax.rem(t, count), lambda copy: copy.wait_send())
        return carry

    lax.fori_loop(0, rep_size * count, drain, 0)
    for j, b in own_chunks:
        send_chunk(j, b, lambda copy: copy.wait_send())


def local(sizes, prompts, frozen_projection_weight, lowrank_down_factor, lowrank_up_factor, magnitude):
    tp_size, dp_size, rep_size = sizes
    layers, rows, columns = frozen_projection_weight.shape
    rank = lowrank_down_factor.shape[2]
    tokens = prompts.shape[0]
    blocks = dp_size * rep_size
    y_size = dp_size // 2
    count = 2 * layers
    dma = pltpu.SemaphoreType.DMA
    return pl.pallas_call(
        functools.partial(kernel, sizes),
        out_shape=jax.ShapeDtypeStruct((layers, tokens, columns), jnp.bfloat16),
        in_specs=[pl.BlockSpec(memory_space=pl.ANY)] * 4 + [pl.BlockSpec(memory_space=pltpu.VMEM)],
        out_specs=pl.BlockSpec(memory_space=pltpu.VMEM),
        scratch_shapes=[
            pltpu.VMEM((blocks, layers, rows, columns), jnp.bfloat16),
            pltpu.VMEM((blocks, tokens, rows), jnp.bfloat16),
            pltpu.VMEM((layers, rank, rows), jnp.bfloat16),
            pltpu.VMEM((layers, rank, columns), jnp.bfloat16),
            pltpu.VMEM((layers, tokens, columns), jnp.float32),
            pltpu.VMEM((layers, 8, columns), jnp.float32),
            dma((blocks * count,)),
            dma((y_size * rep_size * count,)),
            dma((y_size * rep_size * count,)),
            dma((max(1, (y_size - 1) * rep_size * count),)),
            dma((y_size * rep_size * count,)),
            dma((max(1, (tp_size - 1) * blocks),)),
            dma((blocks,)),
            dma((blocks,)),
            dma((count,)),
            dma((2,)),
        ],
        compiler_params=pltpu.CompilerParams(
            collective_id=0, has_side_effects=True, vmem_limit_bytes=66_000_000
        ),
        cost_estimate=pl.CostEstimate(
            flops=2 * layers * tokens * columns * rows * blocks, bytes_accessed=2 * blocks * rows * columns,
            transcendentals=0,
        ),
    )(prompts, frozen_projection_weight, jnp.swapaxes(lowrank_down_factor, 1, 2), lowrank_up_factor, magnitude)


def solution(mesh):
    in_specs = (
        P(("dp", "rep"), "tp"),
        P(None, ("dp", "rep"), "tp"),
        P(None, ("dp", "rep"), None),
        P(None, None, "tp"),
        P(None, "tp"),
    )
    out_specs = P(None, ("dp", "rep"), "tp")
    sizes = tuple(mesh.shape[name] for name in ("tp", "dp", "rep"))
    return jax.shard_map(
        functools.partial(local, sizes), mesh=mesh, in_specs=in_specs, out_specs=out_specs, check_vma=False
    )
```

time: 199 us -> 180 us (0.905)
  Pallas kernels: 188 us -> 174 us
  other arithmetic: 6.27 us -> 0 us
  matrix products: 3.74 us -> 0 us
  local copies, waits for them, and re-layouts: 0.95 us -> 3.86 us
    pallas_call x1, Pallas kernels: 188 us -> 174 us  [local(): pl.pallas_call(functools.partial(kernel, sizes), out_shape=jax.ShapeDtype...]
    convert_element_type x1 -> x0, other arithmetic: 5.39 us -> none  [local(): return (product * factor[:, None, :]).astype(jnp.bfloat16)]
    dot_general x1 -> x0, matrix products: 3.74 us -> none  [merge_rows(): jnp.einsum('lrk,lkc->lrc', down_rows, up_matrix, preferred_element_type=j...]
    unnamed x4 -> x1, local copies, waits for them, and re-layouts: 0.95 us -> 3.86 us
where the time goes in v1:
time: 180 us; the launch traced here: 178 us
  Pallas kernels  174 us (97%)
  local copies, waits for them, and re-layouts  3.86 us (2%)
    pallas_call x1, Pallas kernels, local(): pl.pallas_call(functools.partial(kernel, sizes), out_shape=jax.ShapeDtype...  174 us
    unnamed x1, local copies, waits for them, and re-layouts  3.86 us

profile of v1, /device:TPU:1, one launch (start us, length us, event | category | flops | bytes accessed | tf_op | source)
XLA Modules:
  0.0 178.1 jit_solution(3210017136538779146)
XLA Ops:
  0.0 174.2 %shard_map.55 = bf16[2,768,1024]{2,1,0:T(8,128)(2,1)} custom-call(bf16[768,4096]{1,0:T(8,128)(2,1)} %prompts_ref.1, bf16[2,512,1024]{2,1,0:T(8,128)(2,1)} %weight_ref.1, bf16[2,64,512]{2,1,0:T(8,128)(2,1)} %bitcast.1, bf16[2,64,1024]{2,1,0:T(8,128)(2,1)} %up_ref.1, f32[2,1024]{1,0:T(2,128)} %magnitude_ref.1), custom_call_target="tpu_custom_call" | custom-call | flops 25769803776 | bytes 16777216 | tf_op jit(solution)/shard_map/pallas_call | solution.py:336
  174.3 3.9 %copy.7 = bf16[2,768,1024]{2,1,0:T(8,128)(2,1)} copy(bf16[2,768,1024]{2,1,0:T(8,128)(2,1)} %shard_map.55) | data formatting | bytes 6291456

commit v2 on v1

--- a/solution.py
+++ b/solution.py
@@ -21,6 +21,7 @@
     layers, rows, columns = weight_ref.shape
     tokens = prompts_ref.shape[0]
     half = rows // 2
+    width = columns // 2
     count = 2 * layers
     groups = dp_size // tp_size
     x = lax.axis_index("tp")
@@ -37,9 +38,9 @@
     def block(yy, cc, zz):
         return (yy * 2 + cc) * rep_size + zz
 
-    def piece(b, k):
+    def piece(b, k, h):
         start = pl.multiple_of(k // layers * half, half)
-        return wbuf.at[b, lax.rem(k, layers), pl.ds(start, half), :]
+        return wbuf.at[b, lax.rem(k, layers), pl.ds(start, half), pl.ds(h * width, width)]
 
     def ranked(at):
         longer = -1 if at > last - at else 1
@@ -69,14 +70,14 @@
             device_id=device, device_id_type=MESH,
         )
 
-    def wait_piece(b, k):
-        remote(piece(b, k), csend.at[0], arrive.at[b * count + k], partner).wait_recv()
-
-    def copies(o, zz, k, act):
+    def wait_piece(b, k, h):
+        remote(piece(b, k, h), csend.at[0], arrive.at[(b * count + k) * 2 + h], partner).wait_recv()
+
+    def copies(o, zz, k, h, act):
         yy = column(o)
         b = block(yy, c, zz)
-        ref, landed = piece(b, k), arrive.at[b * count + k]
-        at = (yy * rep_size + zz) * count + k
+        ref, landed = piece(b, k, h), arrive.at[(b * count + k) * 2 + h]
+        at = ((yy * rep_size + zz) * count + k) * 2 + h
         onz = doubled(zz, k)
         along = onz if o > 0 else (z >= 0)
 
@@ -92,23 +93,24 @@
             for p in range(1, y_size):
                 @pl.when((zz == z) | jnp.logical_not(onz))
                 def _(p=p):
-                    act(remote(ref, ysend.at[((p - 1) * rep_size + zz) * count + k], landed, y_device(p)))
+                    act(remote(ref, ysend.at[(((p - 1) * rep_size + zz) * count + k) * 2 + h], landed, y_device(p)))
 
         act(remote(ref, csend.at[at], landed, partner))
 
-    def forward(o, zz, k):
-        copies(o, zz, k, lambda copy: copy.start())
-
-    def duty(o, zz, k):
-        wait_piece(block(column(o), c, zz), k)
-        forward(o, zz, k)
+    def forward(o, zz, k, h):
+        copies(o, zz, k, h, lambda copy: copy.start())
+
+    def duty(o, zz, k, halves=(0, 1)):
+        for h in halves:
+            wait_piece(block(column(o), c, zz), k, h)
+            forward(o, zz, k, h)
 
     me = block(y, c, z)
 
     def load_weight(k):
-        start = k // layers * half
+        at = pl.ds(k // layers * half, half)
         return pltpu.make_async_copy(
-            weight_ref.at[k % layers, pl.ds(start, half), :], piece(me, jnp.int32(k)), load_w.at[k]
+            weight_ref.at[k % layers, at, :], wbuf.at[me, k % layers, at, :], load_w.at[k]
         )
 
     load_down = pltpu.make_async_copy(down_ref, dbuf, load_f.at[0])
@@ -150,7 +152,7 @@
 
     load_down.wait()
     load_up.wait()
-    tile = min(256, columns)
+    tile = min(512, columns)
 
     def merge(k):
         layer, start = k % layers, k // layers * half
@@ -170,28 +172,32 @@
 
     neighbours = jnp.where(z > 0, 1, 0) + jnp.where(z < last, 1, 0)
 
-    def send_chunk(j, b, act):
+    def send_chunk(n, act):
+        j, b = own_chunks[n]
         for o in range(1, tp_size):
             act(
                 remote(
-                    pbuf.at[b], psend.at[(o - 1) * dp_size * rep_size + b], parrive.at[b],
+                    pbuf.at[b], psend.at[(o - 1) * len(own_chunks) + n], parrive.at[b],
                     {"tp": lax.rem(x + o, tp_size), "dp": d, "rep": z},
                 )
             )
+
+    def start_chunk(n):
+        load_chunk(*own_chunks[n]).wait()
+        send_chunk(n, lambda copy: copy.start())
 
     for k in range(count):
         merge(k)
         if k == 0:
             pl.semaphore_wait(barrier, neighbours + (1 + y_size - 1 + tp_size - 1))
         else:
-            forward(0, z, jnp.int32(k - 1))
-    for j, b in own_chunks[:1]:
-        load_chunk(j, b).wait()
-        send_chunk(j, b, lambda copy: copy.start())
-    forward(0, z, jnp.int32(count - 1))
-    for j, b in own_chunks[1:]:
-        load_chunk(j, b).wait()
-        send_chunk(j, b, lambda copy: copy.start())
+            for h in range(2):
+                forward(0, z, jnp.int32(k - 1), h)
+    start_chunk(0)
+    for h in range(2):
+        forward(0, z, jnp.int32(count - 1), h)
+    for n in range(1, len(own_chunks)):
+        start_chunk(n)
 
     acc[...] = jnp.zeros_like(acc)
     squares[...] = jnp.zeros_like(squares)
@@ -201,33 +207,34 @@
         def _():
             remote(pbuf.at[b], psend.at[0], parrive.at[b], partner).wait_recv()
 
-    def compute(b, k):
-        layer = lax.rem(k, layers)
-        at = pl.ds(pl.multiple_of(k // layers * half, half), half)
-        weight = wbuf[b, layer, at, :]
-        acc[layer] += jnp.dot(pbuf[b, :, at], weight, preferred_element_type=jnp.float32)
+    def compute(b, layer, at, cols):
+        weight = wbuf[b, layer, at, cols]
+        acc[layer, :, cols] += jnp.dot(pbuf[b, :, at], weight, preferred_element_type=jnp.float32)
         wide = weight.astype(jnp.float32)
-        squares[layer] += jnp.sum((wide * wide).reshape(half // 8, 8, columns), axis=0)
+        squares[layer, :, cols] += jnp.sum((wide * wide).reshape(-1, 8, wide.shape[1]), axis=0)
 
     def blocks_of(q, zz):
         return block(column(q // 2), lax.rem(c + q, 2), zz)
 
-    def consume(zz, k, first, end, fresh):
+    def consume(zz, k, fresh):
+        at = pl.ds(pl.multiple_of(k // layers * half, half), half)
+
         def step(q, carry):
             b = blocks_of(q, zz)
-            if fresh is not None:
-                @pl.when(fresh)
-                def _():
-                    wait_chunk(b)
+
+            @pl.when(fresh)
+            def _():
+                wait_chunk(b)
 
             @pl.when(lax.rem(q, 2) == 1)
             def _():
-                wait_piece(b, k)
-
-            compute(b, k)
+                for h in range(2):
+                    wait_piece(b, k, h)
+
+            compute(b, lax.rem(k, layers), at, slice(None))
             return carry
 
-        lax.fori_loop(first, end, step, 0)
+        lax.fori_loop(0, 2 * y_size, step, 0)
 
     total = last * count
 
@@ -266,7 +273,7 @@
             for o in range(1, y_size):
                 duty(o, zz, k)
 
-        consume(zz, k, 0, 2 * y_size, k == 0)
+        consume(zz, k, k == 0)
         return carry
 
     lax.fori_loop(0, total, substep, 0)
@@ -275,53 +282,73 @@
     for q in range(2 * y_size):
         wait_chunk(blocks_of(q, far))
 
-    def early(k, carry):
-        consume(far, k, 0, 2, None)
+    def drain(zz, k):
+        for o in range(y_size):
+            for h in range(2):
+                copies(o, zz, k, h, lambda copy: copy.wait_send())
+
+    def drain_plane(t, carry):
+        drain(plane(t // count), lax.rem(t, count))
         return carry
 
-    lax.fori_loop(0, layers, early, 0)
+    lax.fori_loop(0, total, drain_plane, 0)
+    for n in range(len(own_chunks)):
+        send_chunk(n, lambda copy: copy.wait_send())
     band = min(128, tokens)
 
+    def gather(layer, first, end, halves):
+        cols = pl.ds(halves[0] * width, len(halves) * width)
+
+        def step(q, carry):
+            b = blocks_of(q, far)
+
+            @pl.when(lax.rem(q, 2) == 1)
+            def _():
+                for h in halves:
+                    wait_piece(b, layer, h)
+                    wait_piece(b, layers + layer, h)
+
+            compute(b, layer, slice(None), cols)
+            return carry
+
+        lax.fori_loop(first, end, step, 0)
+
     def finish(layer, carry):
-        def late(part, inner):
-            o_first = jnp.where(part == 0, 0, 2)
-            o_end = jnp.where(part == 0, 2, 2 * y_size)
-            k = jnp.where(part == 2, layer, layers + layer)
-
-            @pl.when((part == 0) & jnp.logical_not(middle))
-            def _():
-                duty(0, far, k)
-
-            @pl.when((part == 2) | ((part == 1) & jnp.logical_not(middle)))
-            def _():
-                for o in range(1, y_size):
-                    duty(o, far, k)
-
-            consume(far, k, o_first, o_end, None)
-            return inner
-
-        lax.fori_loop(0, 3, late, 0)
-        norm = jnp.sqrt(jnp.sum(squares[layer], axis=0, keepdims=True) + epsilon)
-        factor = magnitude_ref[pl.ds(layer, 1), :] / norm
-
-        def scale(t, inner):
-            at = pl.ds(pl.multiple_of(t * band, band), band)
-            out_ref[layer, at, :] = (acc[layer, at, :] * factor).astype(out_ref.dtype)
-            return inner
-
-        lax.fori_loop(0, tokens // band, scale, 0)
+        @pl.when(jnp.logical_not(middle))
+        def _():
+            duty(0, far, layers + layer)
+
+        gather(layer, 0, 2, (0, 1))
+
+        @pl.when(layer > 0)
+        def _():
+            drain(far, layer - 1)
+            drain(far, layers + layer - 1)
+
+        for h in range(2):
+            for o in range(1, y_size):
+                duty(o, far, layer, (h,))
+
+                @pl.when(jnp.logical_not(middle))
+                def _(o=o):
+                    duty(o, far, layers + layer, (h,))
+
+            gather(layer, 2, 2 * y_size, (h,))
+            cols = pl.ds(h * width, width)
+            norm = jnp.sqrt(jnp.sum(squares[layer, :, cols], axis=0, keepdims=True) + epsilon)
+            factor = magnitude_ref[pl.ds(layer, 1), :][:, h * width:(h + 1) * width] / norm
+
+            def scale(t, inner, cols=cols, factor=factor):
+                at = pl.ds(pl.multiple_of(t * band, band), band)
+                out_ref[layer, at, cols] = (acc[layer, at, cols] * factor).astype(out_ref.dtype)
+                return inner
+
+            lax.fori_loop(0, tokens // band, scale, 0)
         return carry
 
     lax.fori_loop(0, layers, finish, 0)
-
-    def drain(t, carry):
-        for o in range(y_size):
-            copies(o, t // count, lax.rem(t, count), lambda copy: copy.wait_send())
-        return carry
-
-    lax.fori_loop(0, rep_size * count, drain, 0)
-    for j, b in own_chunks:
-        send_chunk(j, b, lambda copy: copy.wait_send())
+    drain(far, layers - 1)
+    drain(far, count - 1)
 
 
 def local(sizes, prompts, frozen_projection_weight, lowrank_down_factor, lowrank_up_factor, magnitude):
@@ -335,7 +362,7 @@
     dma = pltpu.SemaphoreType.DMA
     return pl.pallas_call(
         functools.partial(kernel, sizes),
-        out_shape=jax.ShapeDtypeStruct((layers, tokens, columns), jnp.bfloat16),
+        out_shape=pltpu.VMEM((layers, tokens, columns), jnp.bfloat16),
         in_specs=[pl.BlockSpec(memory_space=pl.ANY)] * 4 + [pl.BlockSpec(memory_space=pltpu.VMEM)],
         out_specs=pl.BlockSpec(memory_space=pltpu.VMEM),
         scratch_shapes=[
@@ -345,19 +372,19 @@
             pltpu.VMEM((layers, rank, columns), jnp.bfloat16),
             pltpu.VMEM((layers, tokens, columns), jnp.float32),
             pltpu.VMEM((layers, 8, columns), jnp.float32),
-            dma((blocks * count,)),
-            dma((y_size * rep_size * count,)),
-            dma((y_size * rep_size * count,)),
-            dma((max(1, (y_size - 1) * rep_size * count),)),
-            dma((y_size * rep_size * count,)),
-            dma((max(1, (tp_size - 1) * blocks),)),
+            dma((blocks * count * 2,)),
+            dma((y_size * rep_size * count * 2,)),
+            dma((y_size * rep_size * count * 2,)),
+            dma((max(1, (y_size - 1) * rep_size * count * 2),)),
+            dma((y_size * rep_size * count * 2,)),
+            dma((max(1, (tp_size - 1) * (blocks // tp_size)),)),
             dma((blocks,)),
             dma((blocks,)),
             dma((count,)),
             dma((2,)),
         ],
         compiler_params=pltpu.CompilerParams(
-            collective_id=0, has_side_effects=True, vmem_limit_bytes=66_000_000
+            collective_id=0, has_side_effects=True, vmem_limit_bytes=58_000_000
         ),
         cost_estimate=pl.CostEstimate(
             flops=2 * layers * tokens * columns * rows * blocks, bytes_accessed=2 * blocks * rows * columns,

time: 180 us -> 173 us (0.961); the launches traced: 178 us -> 173 us
  Pallas kernels: 174 us -> 171 us
  local copies, waits for them, and re-layouts: 3.86 us -> 1.67 us
    pallas_call x1, Pallas kernels: 174 us -> 171 us  [local(): pl.pallas_call(functools.partial(kernel, sizes), out_shape=pltpu.VMEM((la...]
    unnamed x1, local copies, waits for them, and re-layouts: 3.86 us -> 1.67 us
where the time goes in v2:
time: 173 us
  Pallas kernels  171 us (99%)
    pallas_call x1, Pallas kernels, local(): pl.pallas_call(functools.partial(kernel, sizes), out_shape=pltpu.VMEM((la...  171 us

profile of v2, /device:TPU:1, one launch (start us, length us, event | category | flops | bytes accessed | tf_op | source)
XLA Modules:
  0.0 173.0 jit_solution(15485524995024938990)
XLA Ops:
  0.0 171.4 %shard_map.55 = bf16[2,768,1024]{2,1,0:T(8,128)(2,1)S(1)} custom-call(bf16[768,4096]{1,0:T(8,128)(2,1)} %prompts_ref.1, bf16[2,512,1024]{2,1,0:T(8,128)(2,1)} %weight_ref.1, bf16[2,64,512]{2,1,0:T(8,128)(2,1)} %bitcast.1, bf16[2,64,1024]{2,1,0:T(8,128)(2,1)} %up_ref.1, f32[2,1024]{1,0:T(2,128)} %magnitude_ref.1), custom_call_target="tpu_custom_call" | custom-call | flops 25769803776 | bytes 16777216 | tf_op jit(solution)/shard_map/pallas_call | solution.py:363
  171.4 1.7 copy.7

commit v3 on v2

--- a/solution.py
+++ b/solution.py
@@ -13,7 +13,7 @@
 
 def kernel(
     sizes, prompts_ref, weight_ref, down_ref, up_ref, magnitude_ref, out_ref,
-    wbuf, pbuf, dbuf, ubuf, acc, squares,
+    wbuf, pbuf, dbuf, ubuf, mbuf, acc, squares,
     arrive, zup, zdown, ysend, csend, psend, parrive, load_p, load_w, load_f,
 ):
     tp_size, dp_size, rep_size = sizes
@@ -115,23 +115,13 @@
 
     load_down = pltpu.make_async_copy(down_ref, dbuf, load_f.at[0])
     load_up = pltpu.make_async_copy(up_ref, ubuf, load_f.at[1])
+    load_magnitude = pltpu.make_async_copy(magnitude_ref, mbuf, load_f.at[2])
+    load_weight(0).start()
     load_down.start()
     load_up.start()
-    for k in range(count):
+    for k in range(1, count):
         load_weight(k).start()
-
-    own_chunks = []
-    for i in range(rep_size):
-        for g in range(groups):
-            zz = plane(i)
-            own_chunks.append((g * rep_size + zz, x * groups * rep_size + g * rep_size + zz))
-
-    def load_chunk(j, b):
-        start = pl.multiple_of(j * rows, rows)
-        return pltpu.make_async_copy(prompts_ref.at[:, pl.ds(start, rows)], pbuf.at[b], load_p.at[b])
-
-    for j, b in own_chunks:
-        load_chunk(j, b).start()
+    load_magnitude.start()
 
     barrier = pltpu.get_barrier_semaphore()
     pl.semaphore_signal(barrier, 1, device_id=partner, device_id_type=MESH)
@@ -149,6 +139,16 @@
     @pl.when(z < last)
     def _():
         pl.semaphore_signal(barrier, 1, device_id=z_device(1), device_id_type=MESH)
+
+    own_chunks = []
+    for i in range(rep_size):
+        for g in range(groups):
+            zz = plane(i)
+            own_chunks.append((g * rep_size + zz, x * groups * rep_size + g * rep_size + zz))
+
+    def load_chunk(j, b):
+        start = pl.multiple_of(j * rows, rows)
+        return pltpu.make_async_copy(prompts_ref.at[:, pl.ds(start, rows)], pbuf.at[b], load_p.at[b])
 
     load_down.wait()
     load_up.wait()
@@ -189,6 +189,8 @@
     for k in range(count):
         merge(k)
         if k == 0:
+            for j, b in own_chunks:
+                load_chunk(j, b).start()
             pl.semaphore_wait(barrier, neighbours + (1 + y_size - 1 + tp_size - 1))
         else:
             for h in range(2):
@@ -278,6 +280,7 @@
 
     lax.fori_loop(0, total, substep, 0)
 
+    load_magnitude.wait()
     far = plane(last)
     for q in range(2 * y_size):
         wait_chunk(blocks_of(q, far))
@@ -336,7 +339,7 @@
             gather(layer, 2, 2 * y_size, (h,))
             cols = pl.ds(h * width, width)
             norm = jnp.sqrt(jnp.sum(squares[layer, :, cols], axis=0, keepdims=True) + epsilon)
-            factor = magnitude_ref[pl.ds(layer, 1), :][:, h * width:(h + 1) * width] / norm
+            factor = mbuf[pl.ds(layer, 1), :][:, h * width:(h + 1) * width] / norm
 
             def scale(t, inner, cols=cols, factor=factor):
                 at = pl.ds(pl.multiple_of(t * band, band), band)
@@ -363,13 +366,14 @@
     return pl.pallas_call(
         functools.partial(kernel, sizes),
         out_shape=pltpu.VMEM((layers, tokens, columns), jnp.bfloat16),
-        in_specs=[pl.BlockSpec(memory_space=pl.ANY)] * 4 + [pl.BlockSpec(memory_space=pltpu.VMEM)],
+        in_specs=[pl.BlockSpec(memory_space=pl.ANY)] * 5,
         out_specs=pl.BlockSpec(memory_space=pltpu.VMEM),
         scratch_shapes=[
             pltpu.VMEM((blocks, layers, rows, columns), jnp.bfloat16),
             pltpu.VMEM((blocks, tokens, rows), jnp.bfloat16),
             pltpu.VMEM((layers, rank, rows), jnp.bfloat16),
             pltpu.VMEM((layers, rank, columns), jnp.bfloat16),
+            pltpu.VMEM((layers, columns), jnp.float32),
             pltpu.VMEM((layers, tokens, columns), jnp.float32),
             pltpu.VMEM((layers, 8, columns), jnp.float32),
             dma((blocks * count * 2,)),
@@ -381,10 +385,10 @@
             dma((blocks,)),
             dma((blocks,)),
             dma((count,)),
-            dma((2,)),
+            dma((3,)),
         ],
         compiler_params=pltpu.CompilerParams(
-            collective_id=0, has_side_effects=True, vmem_limit_bytes=58_000_000
+            collective_id=0, has_side_effects=True, vmem_limit_bytes=61_000_000
         ),
         cost_estimate=pl.CostEstimate(
             flops=2 * layers * tokens * columns * rows * blocks, bytes_accessed=2 * blocks * rows * columns,

time: 173 us -> 171 us (0.988)
  Pallas kernels: 171 us -> 169 us
    pallas_call x1, Pallas kernels: 171 us -> 169 us  [local(): pl.pallas_call(functools.partial(kernel, sizes), out_shape=pltpu.VMEM((la...]
where the time goes in v3:
time: 171 us
  Pallas kernels  169 us (99%)
    pallas_call x1, Pallas kernels, local(): pl.pallas_call(functools.partial(kernel, sizes), out_shape=pltpu.VMEM((la...  169 us

profile of v3, /device:TPU:1, one launch (start us, length us, event | category | flops | bytes accessed | tf_op | source)
XLA Modules:
  0.0 170.6 jit_solution(12876499787676863706)
XLA Ops:
  0.0 168.9 %shard_map.55 = bf16[2,768,1024]{2,1,0:T(8,128)(2,1)S(1)} custom-call(bf16[768,4096]{1,0:T(8,128)(2,1)} %prompts_ref.1, bf16[2,512,1024]{2,1,0:T(8,128)(2,1)} %weight_ref.1, bf16[2,64,512]{2,1,0:T(8,128)(2,1)} %bitcast.1, bf16[2,64,1024]{2,1,0:T(8,128)(2,1)} %up_ref.1, f32[2,1024]{1,0:T(2,128)} %magnitude_ref.1), custom_call_target="tpu_custom_call" | custom-call | flops 25769803776 | bytes 16777216 | tf_op jit(solution)/shard_map/pallas_call | solution.py:366
  168.9 1.7 copy.7

commit v4 on v3

--- a/solution.py
+++ b/solution.py
@@ -71,34 +71,30 @@
         )
 
     def wait_piece(b, k, h):
-        remote(piece(b, k, h), csend.at[0], arrive.at[(b * count + k) * 2 + h], partner).wait_recv()
-
-    def copies(o, zz, k, h, act):
+        remote(piece(b, k, h), csend, arrive.at[(b * count + k) * 2 + h], partner).wait_recv()
+
+    def forward(o, zz, k, h):
         yy = column(o)
         b = block(yy, c, zz)
         ref, landed = piece(b, k, h), arrive.at[(b * count + k) * 2 + h]
-        at = ((yy * rep_size + zz) * count + k) * 2 + h
         onz = doubled(zz, k)
         along = onz if o > 0 else (z >= 0)
 
         @pl.when(along & (zz >= z) & (z > 0))
         def _():
-            act(remote(ref, zdown.at[at], landed, z_device(-1)))
+            remote(ref, zdown, landed, z_device(-1)).start()
 
         @pl.when(along & (zz <= z) & (z < last))
         def _():
-            act(remote(ref, zup.at[at], landed, z_device(1)))
+            remote(ref, zup, landed, z_device(1)).start()
 
         if o == 0:
             for p in range(1, y_size):
                 @pl.when((zz == z) | jnp.logical_not(onz))
                 def _(p=p):
-                    act(remote(ref, ysend.at[(((p - 1) * rep_size + zz) * count + k) * 2 + h], landed, y_device(p)))
-
-        act(remote(ref, csend.at[at], landed, partner))
-
-    def forward(o, zz, k, h):
-        copies(o, zz, k, h, lambda copy: copy.start())
+                    remote(ref, ysend.at[p - 1], landed, y_device(p)).start()
+
+        remote(ref, csend, landed, partner).start()
 
     def duty(o, zz, k, halves=(0, 1)):
         for h in halves:
@@ -146,9 +142,10 @@
             zz = plane(i)
             own_chunks.append((g * rep_size + zz, x * groups * rep_size + g * rep_size + zz))
 
-    def load_chunk(j, b):
+    def load_chunk(n):
+        j, b = own_chunks[n]
         start = pl.multiple_of(j * rows, rows)
-        return pltpu.make_async_copy(prompts_ref.at[:, pl.ds(start, rows)], pbuf.at[b], load_p.at[b])
+        return pltpu.make_async_copy(prompts_ref.at[:, pl.ds(start, rows)], pbuf.at[b], load_p.at[n])
 
     load_down.wait()
     load_up.wait()
@@ -172,25 +169,20 @@
 
     neighbours = jnp.where(z > 0, 1, 0) + jnp.where(z < last, 1, 0)
 
-    def send_chunk(n, act):
-        j, b = own_chunks[n]
+    def start_chunk(n):
+        load_chunk(n).wait()
+        b = own_chunks[n][1]
         for o in range(1, tp_size):
-            act(
-                remote(
-                    pbuf.at[b], psend.at[(o - 1) * len(own_chunks) + n], parrive.at[b],
-                    {"tp": lax.rem(x + o, tp_size), "dp": d, "rep": z},
-                )
-            )
-
-    def start_chunk(n):
-        load_chunk(*own_chunks[n]).wait()
-        send_chunk(n, lambda copy: copy.start())
+            remote(
+                pbuf.at[b], psend.at[o - 1], parrive.at[b],
+                {"tp": lax.rem(x + o, tp_size), "dp": d, "rep": z},
+            ).start()
 
     for k in range(count):
         merge(k)
         if k == 0:
-            for j, b in own_chunks:
-                load_chunk(j, b).start()
+            for n in range(len(own_chunks)):
+                load_chunk(n).start()
             pl.semaphore_wait(barrier, neighbours + (1 + y_size - 1 + tp_size - 1))
         else:
             for h in range(2):
@@ -285,18 +277,6 @@
     for q in range(2 * y_size):
         wait_chunk(blocks_of(q, far))
 
-    def drain(zz, k):
-        for o in range(y_size):
-            for h in range(2):
-                copies(o, zz, k, h, lambda copy: copy.wait_send())
-
-    def drain_plane(t, carry):
-        drain(plane(t // count), lax.rem(t, count))
-        return carry
-
-    lax.fori_loop(0, total, drain_plane, 0)
-    for n in range(len(own_chunks)):
-        send_chunk(n, lambda copy: copy.wait_send())
     band = min(128, tokens)
 
     def gather(layer, first, end, halves):
@@ -323,11 +303,6 @@
 
         gather(layer, 0, 2, (0, 1))
 
-        @pl.when(layer > 0)
-        def _():
-            drain(far, layer - 1)
-            drain(far, layers + layer - 1)
-
         for h in range(2):
             for o in range(1, y_size):
                 duty(o, far, layer, (h,))
@@ -350,8 +325,37 @@
         return carry
 
     lax.fori_loop(0, layers, finish, 0)
-    drain(far, layers - 1)
-    drain(far, count - 1)
+
+    def sent(amount, sem):
+        ref = wbuf.at[pl.ds(0, amount), 0]
+        remote(ref, sem, arrive.at[0], partner).wait_send()
+
+    for n in range(rep_size):
+        amount = (n + 1) * layers + (y_size - 1) * layers // 2
+
+        if n < last:
+            @pl.when(z == n)
+            def _(amount=amount):
+                sent(amount, zup)
+
+            @pl.when(z == last - n)
+            def _(amount=amount):
+                sent(amount, zdown)
+
+    for p in range(1, y_size):
+        @pl.when(middle)
+        def _(p=p):
+            sent(rep_size * layers - 2 * layers // 2, ysend.at[p - 1])
+
+        @pl.when(jnp.logical_not(middle))
+        def _(p=p):
+            sent(rep_size * layers - layers // 2, ysend.at[p - 1])
+
+    whole = wbuf.at[pl.ds(0, y_size * rep_size)]
+    remote(whole, csend, arrive.at[0], partner).wait_send()
+    for o in range(1, tp_size):
+        chunks = pbuf.at[pl.ds(0, len(own_chunks))]
+        remote(chunks, psend.at[o - 1], arrive.at[0], partner).wait_send()
 
 
 def local(sizes, prompts, frozen_projection_weight, lowrank_down_factor, lowrank_up_factor, magnitude):
@@ -377,13 +381,13 @@
             pltpu.VMEM((layers, tokens, columns), jnp.float32),
             pltpu.VMEM((layers, 8, columns), jnp.float32),
             dma((blocks * count * 2,)),
-            dma((y_size * rep_size * count * 2,)),
-            dma((y_size * rep_size * count * 2,)),
-            dma((max(1, (y_size - 1) * rep_size * count * 2),)),
-            dma((y_size * rep_size * count * 2,)),
-            dma((max(1, (tp_size - 1) * (blocks // tp_size)),)),
+            dma(()),
+            dma(()),
+            dma((max(1, y_size - 1),)),
+            dma(()),
+            dma((max(1, tp_size - 1),)),
             dma((blocks,)),
-            dma((blocks,)),
+            dma((blocks // tp_size,)),
             dma((count,)),
             dma((3,)),
         ],

time: 171 us -> 169 us (0.988)
  Pallas kernels: 169 us -> 167 us
    pallas_call x1, Pallas kernels: 169 us -> 167 us  [local(): pl.pallas_call(functools.partial(kernel, sizes), out_shape=pltpu.VMEM((la...]
where the time goes in v4:
time: 169 us; the launch traced here: 168 us
  Pallas kernels  167 us (99%)
    pallas_call x1, Pallas kernels, local(): pl.pallas_call(functools.partial(kernel, sizes), out_shape=pltpu.VMEM((la...  167 us

profile of v4, /device:TPU:1, one launch (start us, length us, event | category | flops | bytes accessed | tf_op | source)
XLA Modules:
  0.0 168.5 jit_solution(3965038500247396457)
XLA Ops:
  0.0 166.8 %shard_map.55 = bf16[2,768,1024]{2,1,0:T(8,128)(2,1)S(1)} custom-call(bf16[768,4096]{1,0:T(8,128)(2,1)} %prompts_ref.1, bf16[2,512,1024]{2,1,0:T(8,128)(2,1)} %weight_ref.1, bf16[2,64,512]{2,1,0:T(8,128)(2,1)} %bitcast.1, bf16[2,64,1024]{2,1,0:T(8,128)(2,1)} %up_ref.1, f32[2,1024]{1,0:T(2,128)} %magnitude_ref.1), custom_call_target="tpu_custom_call" | custom-call | flops 25769803776 | bytes 16777216 | tf_op jit(solution)/shard_map/pallas_call | solution.py:370
  166.8 1.7 copy.7
